TPU v7x, 32 devices: a 4x4x1 block of a 4x4x8 slice. The times are simulated.
32 devices in a mesh: dp: 1 (over z), ri: 4 (over y), co: 4 (over x), ro: 2 (over core).
Axes of the slice: x: 4, y: 4, z: 1, core: 2. Of those that a mesh axis runs over, the one named last changes fastest.
The devices are a block of a 4x4x8 slice.
Arguments:
- a_mat: bfloat16 [2048, 24576], P(('dp', 'ri', 'ro'), 'co')
- b_mat: bfloat16 [24576, 16384], P(('dp', 'ri', 'ro'), 'co')
Outputs:
- output: bfloat16 [2048, 16384], P(('dp', 'ri', 'ro'), 'co')
All inputs are finite; a program needn't handle non-finite values.
Results may differ from a plain program's by a relative error of at most 0.001.
Values are sent between devices in bfloat16 or wider.
A program may use at most 768 MiB of HBM per device.

v0:
```python
import jax
import jax.numpy as jnp
from jax import lax
from jax.sharding import PartitionSpec as P, NamedSharding


def solution(mesh):
    grid_spec = P(("dp", "ri", "ro"), "co")

    def local_block(a_block, b_block):
        a_rows = lax.all_gather(a_block, "co", axis=1, tiled=True)
        b_cols = lax.all_gather(b_block, ("ri", "ro"), axis=0, tiled=True)
        product = jnp.dot(a_rows, b_cols, preferred_element_type=jnp.float32)
        return product.astype(jnp.bfloat16)

    return jax.shard_map(local_block, mesh=mesh, in_specs=(grid_spec, grid_spec), out_specs=grid_spec, check_vma=False)
```

profile of v0, /device:TPU:97, one launch (start us, length us, event | category | flops | bytes accessed | tf_op | source)
XLA Modules:
  0.0 1069.9 jit_solution(4049202337555633045)
XLA Ops:
  6.5 0.0 all-gather.3.cloned.1.call-start
  6.6 0.7 all-gather.3.cloned.1.call-update
  7.3 0.1 all-gather.5.cloned.1.call-start
  7.4 0.7 all-gather.5.cloned.1.call-update
  8.1 121.0 %all-gather.3.cloned.1.call-done = bf16[256,24576]{1,0:T(8,128)(2,1)} async-done(((bf16[256,6144]{1,0:T(8,128)(2,1)}), bf16[256,24576]{1,0:T(8,128)(2,1)}) %all-gather.3.cloned.1.call-update) | async-done | bytes 12582928 | tf_op jit(solution)/shard_map/all_gather | solution.py:11
  129.2 861.5 %all-gather.5.cloned.1.call-done = bf16[24576,4096]{1,0:T(8,128)(2,1)} async-done(((bf16[3072,4096]{1,0:T(8,128)(2,1)}), bf16[24576,4096]{1,0:T(8,128)(2,1)}) %all-gather.5.cloned.1.call-update) | async-done | bytes 201326608 | tf_op jit(solution)/shard_map/all_gather | solution.py:12
  990.6 72.4 %convolution_convert_fusion = bf16[256,4096]{1,0:T(8,128)(2,1)} fusion(bf16[256,24576]{1,0:T(8,128)(2,1)} %all-gather.3.cloned.1.call-done, bf16[24576,4096]{1,0:T(8,128)(2,1)} %all-gather.5.cloned.1.call-done), kind=kOutput, calls=%fused_computation | convolution fusion | flops 51540656128 | bytes 216006656 | tf_op jit(solution)/shard_map/dot_general | solution.py:13
Async XLA Ops:
  6.5 122.6 %all-gather.3.cloned.1.call-start = ((), (), s32[]{:S(2)}) async-start(), calls=%async_computation | async-start | bytes 15728640 | tf_op jit(solution)/shard_map/all_gather | solution.py:11
  7.3 983.3 %all-gather.5.cloned.1.call-start = ((), (), s32[]{:S(2)}) async-start(), calls=%async_computation.1 | async-start | bytes 226492416 | tf_op jit(solution)/shard_map/all_gather | solution.py:12
Sparse Core Ops, SparseCore 0:
  8.9 120.2 all-gather.2
  130.8 859.8 all-gather.4
where the time goes:
time: 1070 us
  waiting for transfers between devices  984 us (92%)
  matrix products  72.4 us (7%)
  between operations  13.4 us (1%)
    all_gather x1, waiting for transfers between devices, local_block(): b_cols = lax.all_gather(b_block, ('ri', 'ro'), axis=0, tiled=True)  861 us
    all_gather x1, waiting for transfers between devices, local_block(): a_rows = lax.all_gather(a_block, 'co', axis=1, tiled=True)  121 us
    dot_general x1, matrix products, local_block(): product = jnp.dot(a_rows, b_cols, preferred_element_type=jnp.float32)  72.4 us
  transfers between devices with their start and end apart: 2, of which 2 were waited for; matrix products, arithmetic and copies ran while one was open for 0% of the time, Pallas kernels for 0%

commit v1 on v0

v1 whole, which is shorter than its diff:
```python
import functools

import jax
import jax.numpy as jnp
from jax import lax
from jax.experimental import pallas as pl
from jax.experimental.pallas import tpu as pltpu
from jax.sharding import PartitionSpec as P

MESH = pl.DeviceIdType.MESH
HALVES = 2
WIDTH = 512


def kernel(n, a_ref, b_ref, c_ref, b_far, a_all, b_panel, far_out, far_in, near_out, near_in, own, result,
           a1_send, a1_recv, a2_send, a2_recv, local_sem, b_send, b_recv, load_sem,
           far_send, far_recv, near_send, near_recv, result_sem):
    y, x, core = lax.axis_index("ri"), lax.axis_index("co"), lax.axis_index("ro")
    rows, depth = a_ref.shape
    part = depth // n
    half_k = b_ref.shape[0]
    panels = b_ref.shape[1] // WIDTH
    piece = rows // HALVES
    diagonal = x == y

    def wrap(v):
        return lax.rem(v, n)

    def slot_of(off):
        return off // 2 + 2 * (1 - off % 2)

    def cols(q):
        return pl.ds(pl.multiple_of(q * part, 128), part)

    def panel_cols(p):
        return pl.ds(pl.multiple_of(p * WIDTH, 128), WIDTH)

    def lines(h):
        return pl.ds(h * piece, piece)

    def order(i):
        return i // 2 + (panels // 2) * lax.rem(i, 2)

    bar = pltpu.get_barrier_semaphore()

    def greet(**to):
        pl.semaphore_signal(bar, 1, device_id=to, device_id_type=MESH)

    for off in range(1, n):
        greet(ri=wrap(y + off), co=y)
    @pl.when(jnp.logical_not(diagonal))
    def _():
        greet(ri=y, co=y)
    for delta in range(1, n):
        greet(co=wrap(x + delta))
    greet(ri=wrap(y + 1))
    greet(ri=wrap(y + n - 1))
    greet(ro=1 - core)
    @pl.when(diagonal)
    def _():
        pl.semaphore_wait(bar, 2 * n + 1)
    @pl.when(jnp.logical_not(diagonal))
    def _():
        pl.semaphore_wait(bar, 2 * n + 2)

    my_slot = slot_of(wrap(y - x + n))

    def a1_copy(h, dq, slot):
        q = wrap(x + dq)
        return pltpu.make_async_remote_copy(
            a_ref.at[lines(h), cols(q)], a_all.at[slot, lines(h), cols(q)],
            a1_send.at[h, dq], a1_recv.at[slot, h], device_id={"ri": x, "co": q}, device_id_type=MESH)

    def a1_local(h):
        return pltpu.make_async_copy(a_ref.at[lines(h), cols(x)], a_all.at[2, lines(h), cols(x)], local_sem.at[h])

    for h in range(HALVES):
        @pl.when(diagonal)
        def _():
            a1_local(h).start()
        @pl.when(jnp.logical_not(diagonal))
        def _():
            a1_copy(h, 0, my_slot).start()
        for dq in (1, 3, 2):
            a1_copy(h, dq, my_slot).start()

    def b_copy(p):
        return pltpu.make_async_remote_copy(
            b_ref.at[:, panel_cols(p)], b_far.at[:, panel_cols(p)], b_send.at[p], b_recv.at[p],
            device_id={"ro": 1 - core}, device_id_type=MESH)

    for i in range(panels):
        b_copy(order(jnp.int32(i))).start()

    def near_load(p, s):
        return pltpu.make_async_copy(
            b_ref.at[:, panel_cols(p)], b_panel.at[s, pl.ds(pl.multiple_of(core * half_k, 128), half_k), :], load_sem.at[0, s])

    def far_load(p, s):
        return pltpu.make_async_copy(
            b_far.at[:, panel_cols(p)], b_panel.at[s, pl.ds(pl.multiple_of((1 - core) * half_k, 128), half_k), :], load_sem.at[1, s])

    near_load(0, 0).start()

    def a2_copy(slot, h, delta):
        return pltpu.make_async_remote_copy(
            a_all.at[slot, lines(h), cols(x)], a_all.at[slot, lines(h), cols(x)],
            a2_send.at[slot, h, delta - 1], a2_recv.at[slot, h, delta - 1],
            device_id={"co": wrap(x + delta)}, device_id_type=MESH)

    for slot, h in [(3, h) for h in range(HALVES)] + [(s, h) for h in range(HALVES) for s in (0, 1)] + [(2, h) for h in range(HALVES)]:
        if slot == 2:
            @pl.when(diagonal)
            def _():
                a1_local(h).wait()
            @pl.when(jnp.logical_not(diagonal))
            def _():
                a1_copy(h, 0, slot).wait_recv()
        else:
            a1_copy(h, 0, slot).wait_recv()
        for delta in (1, 3, 2):
            a2_copy(slot, h, delta).start()

    b_copy(0).wait_recv()
    far_load(0, 0).start()

    def far_copy(h, p):
        return pltpu.make_async_remote_copy(
            far_out.at[h, p], far_in.at[h, p], far_send.at[h, p], far_recv.at[h, p],
            device_id={"ri": wrap(y + n - 1 - 2 * (p // (panels // 2)) + n)}, device_id_type=MESH)

    def near_copy(j, h, p):
        return pltpu.make_async_remote_copy(
            near_out.at[j, h, p], near_in.at[j, h, p], near_send.at[j, h, p], near_recv.at[j, h, p],
            device_id={"ri": wrap(y + 1 + (n - 2) * j)}, device_id_type=MESH)

    def send(kind, h, p):
        if kind == "far":
            far_copy(h, p).start()
        elif kind == "near":
            near_copy(0, h, p).start()
            near_copy(1, h, p).start()

    units = [("far", h) for h in range(HALVES)] + [("near", h) for h in range(HALVES)] + [("own", 0)]
    for u, (kind, h) in enumerate(units):
        waits = {"far": [(3, h)], "near": [(0, h), (1, h)], "own": [(2, g) for g in range(HALVES)]}[kind]
        for slot, g in waits:
            for delta in (1, 3, 2):
                a2_copy(slot, g, delta).wait_recv()

        def step(i, _, u=u, kind=kind, h=h):
            p, s = order(i), lax.rem(i, 2)
            if u + 1 < len(units):
                more = i >= 0
            else:
                more = i + 1 < panels
            p1 = order(lax.rem(i + 1, panels))

            @pl.when(more)
            def _():
                near_load(p1, 1 - s).start()
                if u == 0:
                    @pl.when(i + 1 < panels)
                    def _():
                        b_copy(p1).wait_recv()
                far_load(p1, 1 - s).start()
            near_load(p, s).wait()
            far_load(p, s).wait()
            if kind == "near":
                lhs = a_all[0:2, h * piece:(h + 1) * piece].reshape(2 * piece, depth)
            elif kind == "far":
                lhs = a_all[3, h * piece:(h + 1) * piece]
            else:
                lhs = a_all[2]
            value = jnp.dot(lhs, b_panel[s], preferred_element_type=jnp.float32)
            @pl.when(i > 0)
            def _():
                send(kind, h, order(i - 1))
            if u > 0:
                @pl.when(i == 0)
                def _():
                    send(*units[u - 1], panels - 1)
            if kind == "far":
                far_out[h, p] = value
            elif kind == "near":
                near_out[0, h, p] = value[:piece]
                near_out[1, h, p] = value[piece:]
                far_copy(h, p).wait_recv()
                j = 1 - p // (panels // 2)
                near_out[j, h, p] += far_in[h, p]
            else:
                own[:, panel_cols(p)] = value
            return 0

        lax.fori_loop(0, panels, step, 0)

    def result_copy(p):
        return pltpu.make_async_copy(result.at[:, panel_cols(p)], c_ref.at[:, panel_cols(p)], result_sem.at[p])

    def finish(i, _):
        p = order(i)
        for h in range(HALVES):
            near_copy(0, h, p).wait_recv()
            near_copy(1, h, p).wait_recv()
            total = own[h * piece:(h + 1) * piece, panel_cols(p)] + near_in[0, h, p] + near_in[1, h, p]
            result[h * piece:(h + 1) * piece, panel_cols(p)] = total.astype(jnp.bfloat16)
        @pl.when(i > 0)
        def _():
            result_copy(order(i - 1)).start()
        return 0

    lax.fori_loop(0, panels, finish, 0)

    for h in range(HALVES):
        @pl.when(jnp.logical_not(diagonal))
        def _():
            a1_copy(h, 0, my_slot).wait_send()
        for dq in (1, 3, 2):
            a1_copy(h, dq, my_slot).wait_send()
        for slot in range(n):
            for delta in (1, 3, 2):
                a2_copy(slot, h, delta).wait_send()

    def drain(p, _):
        b_copy(p).wait_send()
        for h in range(HALVES):
            far_copy(h, p).wait_send()
            near_copy(0, h, p).wait_send()
            near_copy(1, h, p).wait_send()
        return 0

    lax.fori_loop(0, panels, drain, 0)
    result_copy(panels - 1).start()

    def drain_result(p, _):
        result_copy(p).wait()
        return 0

    lax.fori_loop(0, panels, drain_result, 0)


def solution(mesh):
    n = mesh.shape["ri"]
    spec = P(("dp", "ri", "ro"), "co")

    def block(a, b):
        rows, depth = a.shape
        half_k, width = b.shape
        panels, piece = width // WIDTH, rows // HALVES
        f32, bf16 = jnp.float32, jnp.bfloat16
        dma = pltpu.SemaphoreType.DMA
        hbm = pl.BlockSpec(memory_space=pl.ANY)
        c, _ = pl.pallas_call(
            functools.partial(kernel, n),
            out_shape=(jax.ShapeDtypeStruct((rows, width), bf16), jax.ShapeDtypeStruct((half_k, width), bf16)),
            in_specs=[hbm, hbm],
            out_specs=(hbm, hbm),
            scratch_shapes=[
                pltpu.VMEM((n, rows, depth), bf16),
                pltpu.VMEM((2, 2 * half_k, WIDTH), bf16),
                pltpu.VMEM((HALVES, panels, piece, WIDTH), f32),
                pltpu.VMEM((HALVES, panels, piece, WIDTH), f32),
                pltpu.VMEM((2, HALVES, panels, piece, WIDTH), f32),
                pltpu.VMEM((2, HALVES, panels, piece, WIDTH), f32),
                pltpu.VMEM((rows, width), f32),
                pltpu.VMEM((rows, width), bf16),
                dma((HALVES, n)), dma((n, HALVES)), dma((n, HALVES, n - 1)), dma((n, HALVES, n - 1)), dma((HALVES,)),
                dma((panels,)), dma((panels,)), dma((2, 2)),
                dma((HALVES, panels)), dma((HALVES, panels)), dma((2, HALVES, panels)), dma((2, HALVES, panels)),
                dma((panels,)),
            ],
            compiler_params=pltpu.CompilerParams(
                collective_id=0, has_side_effects=True, vmem_limit_bytes=63 * 2**20),
        )(a, b)
        return c

    return jax.shard_map(block, mesh=mesh, in_specs=(spec, spec), out_specs=spec, check_vma=False)
```

time: 1070 us -> 231 us (0.22)
  the two profiles are of different devices: /device:TPU:97 before, /device:TPU:102 now
where the time goes in v1:
time: 231 us
  Pallas kernels  228 us (99%)
  local copies, waits for them, and re-layouts  3.13 us (1%)
    pallas_call x1, Pallas kernels, block(): pl.pallas_call(functools.partial(kernel, n), out_shape=(jax.ShapeDtypeStr...  228 us

profile of v1, /device:TPU:102, one launch (start us, length us, event | category | flops | bytes accessed | tf_op | source)
XLA Modules:
  0.0 231.1 jit_solution(61408424248878274)
XLA Ops:
  0.0 228.0 %shard_map.28 = (bf16[256,4096]{1,0:T(8,128)(2,1)}, bf16[3072,4096]{1,0:T(8,128)(2,1)}) custom-call(bf16[256,6144]{1,0:T(8,128)(2,1)} %a_ref.1, bf16[3072,4096]{1,0:T(8,128)(2,1)} %b_ref.1), custom_call_target="tpu_custom_call" | custom-call | tf_op jit(solution)/shard_map/pallas_call | solution.py:253
  228.0 3.1 %copy.4 = bf16[256,4096]{1,0:T(8,128)(2,1)} copy(bf16[256,4096]{1,0:T(8,128)(2,1)} %get-tuple-element.6) | data formatting | bytes 4194304

commit v2 on v1

--- a/solution.py
+++ b/solution.py
@@ -12,8 +12,8 @@
 WIDTH = 512
 
 
-def kernel(n, a_ref, b_ref, c_ref, b_far, a_all, b_panel, far_out, far_in, near_out, near_in, own, result,
-           a1_send, a1_recv, a2_send, a2_recv, local_sem, b_send, b_recv, load_sem,
+def kernel(n, a_ref, b_ref, c_ref, b_far, a_all, b_panel, far_out, far_in, near_out, near_in, own, result, a_way,
+           a0_send, a0_recv, a1_send, a1_recv, a2_send, a2_recv, local_sem, b_send, b_recv, load_sem,
            far_send, far_recv, near_send, near_recv, result_sem):
     y, x, core = lax.axis_index("ri"), lax.axis_index("co"), lax.axis_index("ro")
     rows, depth = a_ref.shape
@@ -46,43 +46,49 @@
     def greet(**to):
         pl.semaphore_signal(bar, 1, device_id=to, device_id_type=MESH)
 
-    for off in range(1, n):
-        greet(ri=wrap(y + off), co=y)
-    @pl.when(jnp.logical_not(diagonal))
-    def _():
-        greet(ri=y, co=y)
     for delta in range(1, n):
         greet(co=wrap(x + delta))
-    greet(ri=wrap(y + 1))
-    greet(ri=wrap(y + n - 1))
+        greet(ri=wrap(y + delta))
     greet(ro=1 - core)
-    @pl.when(diagonal)
-    def _():
-        pl.semaphore_wait(bar, 2 * n + 1)
-    @pl.when(jnp.logical_not(diagonal))
-    def _():
-        pl.semaphore_wait(bar, 2 * n + 2)
-
-    my_slot = slot_of(wrap(y - x + n))
-
-    def a1_copy(h, dq, slot):
-        q = wrap(x + dq)
-        return pltpu.make_async_remote_copy(
-            a_ref.at[lines(h), cols(q)], a_all.at[slot, lines(h), cols(q)],
-            a1_send.at[h, dq], a1_recv.at[slot, h], device_id={"ri": x, "co": q}, device_id_type=MESH)
-
-    def a1_local(h):
+    pl.semaphore_wait(bar, 2 * n - 1)
+
+    def a0_copy(h, delta, direct):
+        q = wrap(x + delta)
+        dst = a_all.at[2, lines(h), cols(q)] if direct else a_way.at[delta - 1, h]
+        return pltpu.make_async_remote_copy(
+            a_ref.at[lines(h), cols(q)], dst, a0_send.at[h, delta - 1], a0_recv.at[h, delta - 1],
+            device_id={"co": q}, device_id_type=MESH)
+
+    def a_local(h):
         return pltpu.make_async_copy(a_ref.at[lines(h), cols(x)], a_all.at[2, lines(h), cols(x)], local_sem.at[h])
 
     for h in range(HALVES):
         @pl.when(diagonal)
         def _():
-            a1_local(h).start()
+            a_local(h).start()
+            for delta in (1, 3, 2):
+                a0_copy(h, delta, True).start()
         @pl.when(jnp.logical_not(diagonal))
         def _():
-            a1_copy(h, 0, my_slot).start()
-        for dq in (1, 3, 2):
-            a1_copy(h, dq, my_slot).start()
+            for delta in (1, 3, 2):
+                a0_copy(h, delta, False).start()
+
+    def a1_copy(h, off, src):
+        slot = slot_of(off)
+        return pltpu.make_async_remote_copy(
+            src, a_all.at[slot, lines(h), cols(x)], a1_send.at[h, off - 1], a1_recv.at[slot, h],
+            device_id={"ri": wrap(y - off + n)}, device_id_type=MESH)
+
+    def a1_start(h, off):
+        delta = wrap(x - y + off + n)
+        @pl.when(delta == 0)
+        def _():
+            a1_copy(h, off, a_ref.at[lines(h), cols(x)]).start()
+        for e in range(1, n):
+            @pl.when(delta == e)
+            def _():
+                a0_copy(h, e, False).wait_recv()
+                a1_copy(h, off, a_way.at[e - 1, h]).start()
 
     def b_copy(p):
         return pltpu.make_async_remote_copy(
@@ -102,24 +108,50 @@
 
     near_load(0, 0).start()
 
-    def a2_copy(slot, h, delta):
-        return pltpu.make_async_remote_copy(
-            a_all.at[slot, lines(h), cols(x)], a_all.at[slot, lines(h), cols(x)],
-            a2_send.at[slot, h, delta - 1], a2_recv.at[slot, h, delta - 1],
-            device_id={"co": wrap(x + delta)}, device_id_type=MESH)
-
-    for slot, h in [(3, h) for h in range(HALVES)] + [(s, h) for h in range(HALVES) for s in (0, 1)] + [(2, h) for h in range(HALVES)]:
+    def a2_copy(slot, h, kind):
+        if kind < 2 or kind == 4:
+            view = a_all.at[slot, lines(h), cols(x)]
+        else:
+            view = a_all.at[slot, pl.ds(h * piece + (kind - 2) * (piece // 2), piece // 2), cols(wrap(x + (n - 1, 1)[kind - 2]))]
+        return pltpu.make_async_remote_copy(
+            view, view, a2_send.at[slot, h, kind], a2_recv.at[slot, h, kind],
+            device_id={"co": wrap(x + (1, n - 1, 1, n - 1, 2)[kind])}, device_id_type=MESH)
+
+    def a2_start(slot, h):
         if slot == 2:
             @pl.when(diagonal)
             def _():
-                a1_local(h).wait()
-            @pl.when(jnp.logical_not(diagonal))
-            def _():
-                a1_copy(h, 0, slot).wait_recv()
+                a_local(h).wait()
+            for e in range(1, n):
+                @pl.when(wrap(x - y + n) == e)
+                def _():
+                    a0_copy(h, e, False).wait_recv()
         else:
-            a1_copy(h, 0, slot).wait_recv()
-        for delta in (1, 3, 2):
-            a2_copy(slot, h, delta).start()
+            a1_copy(h, (2 * slot + 1 if slot < 2 else 2), a_way.at[0, h]).wait_recv()
+        a2_copy(slot, h, 0).start()
+        a2_copy(slot, h, 1).start()
+        if slot != 3:
+            a2_copy(slot, h, 4).start()
+
+    def relay(slot, h):
+        for kind in (0, 1):
+            a2_copy(slot, h, kind).wait_recv()
+            a2_copy(slot, h, kind + 2).start()
+
+    for off in (2, 1, 3):
+        a1_start(0, off)
+    a2_start(3, 0)
+    for off in (2, 1, 3):
+        a1_start(1, off)
+    relay(3, 0)
+    a2_start(3, 1)
+
+    hooks = {
+        (0, 1): [lambda: relay(3, 1)],
+        (0, 2): [lambda: a2_start(0, 0), lambda: a2_start(1, 0)],
+        (0, 4): [lambda: a2_start(0, 1), lambda: a2_start(1, 1)],
+        (1, 1): [lambda: a2_start(2, 0), lambda: a2_start(2, 1)],
+    }
 
     b_copy(0).wait_recv()
     far_load(0, 0).start()
@@ -145,8 +177,8 @@
     for u, (kind, h) in enumerate(units):
         waits = {"far": [(3, h)], "near": [(0, h), (1, h)], "own": [(2, g) for g in range(HALVES)]}[kind]
         for slot, g in waits:
-            for delta in (1, 3, 2):
-                a2_copy(slot, g, delta).wait_recv()
+            for k in (2, 3) if slot == 3 else (0, 1, 4):
+                a2_copy(slot, g, k).wait_recv()
 
         def step(i, _, u=u, kind=kind, h=h):
             p, s = order(i), lax.rem(i, 2)
@@ -190,6 +222,12 @@
                 near_out[j, h, p] += far_in[h, p]
             else:
                 own[:, panel_cols(p)] = value
+            for (w, at), work in hooks.items():
+                if w == u:
+                    @pl.when(i == at)
+                    def _(work=work):
+                        for do in work:
+                            do()
             return 0
 
         lax.fori_loop(0, panels, step, 0)
@@ -212,14 +250,12 @@
     lax.fori_loop(0, panels, finish, 0)
 
     for h in range(HALVES):
-        @pl.when(jnp.logical_not(diagonal))
-        def _():
-            a1_copy(h, 0, my_slot).wait_send()
-        for dq in (1, 3, 2):
-            a1_copy(h, dq, my_slot).wait_send()
+        for delta in range(1, n):
+            a0_copy(h, delta, False).wait_send()
+            a1_copy(h, delta, a_way.at[0, h]).wait_send()
         for slot in range(n):
-            for delta in (1, 3, 2):
-                a2_copy(slot, h, delta).wait_send()
+            for kind in (0, 1, 2, 3) if slot == 3 else (0, 1, 4):
+                a2_copy(slot, h, kind).wait_send()
 
     def drain(p, _):
         b_copy(p).wait_send()
@@ -264,7 +300,8 @@
                 pltpu.VMEM((2, HALVES, panels, piece, WIDTH), f32),
                 pltpu.VMEM((rows, width), f32),
                 pltpu.VMEM((rows, width), bf16),
-                dma((HALVES, n)), dma((n, HALVES)), dma((n, HALVES, n - 1)), dma((n, HALVES, n - 1)), dma((HALVES,)),
+                pltpu.VMEM((n - 1, HALVES, piece, depth // n), bf16),
+                dma((HALVES, n - 1)), dma((HALVES, n - 1)), dma((HALVES, n - 1)), dma((n, HALVES)), dma((n, HALVES, 5)), dma((n, HALVES, 5)), dma((HALVES,)),
                 dma((panels,)), dma((panels,)), dma((2, 2)),
                 dma((HALVES, panels)), dma((HALVES, panels)), dma((2, HALVES, panels)), dma((2, HALVES, panels)),
                 dma((panels,)),

time: 231 us -> 208 us (0.900)
  the two profiles are of different devices: /device:TPU:102 before, /device:TPU:97 now
where the time goes in v2:
time: 208 us; the launch traced here: 205 us
  Pallas kernels  202 us (97%)
  local copies, waits for them, and re-layouts  3.13 us (2%)
    pallas_call x1, Pallas kernels, block(): pl.pallas_call(functools.partial(kernel, n), out_shape=(jax.ShapeDtypeStr...  202 us

profile of v2, /device:TPU:97, one launch (start us, length us, event | category | flops | bytes accessed | tf_op | source)
XLA Modules:
  0.0 205.5 jit_solution(10198715681691186159)
XLA Ops:
  0.0 202.4 %shard_map.28 = (bf16[256,4096]{1,0:T(8,128)(2,1)}, bf16[3072,4096]{1,0:T(8,128)(2,1)}) custom-call(bf16[256,6144]{1,0:T(8,128)(2,1)} %a_ref.1, bf16[3072,4096]{1,0:T(8,128)(2,1)} %b_ref.1), custom_call_target="tpu_custom_call" | custom-call | tf_op jit(solution)/shard_map/pallas_call | solution.py:289
  202.4 3.1 %copy.4 = bf16[256,4096]{1,0:T(8,128)(2,1)} copy(bf16[256,4096]{1,0:T(8,128)(2,1)} %get-tuple-element.6) | data formatting | bytes 4194304

commit v3 on v2

--- a/solution.py
+++ b/solution.py
@@ -9,6 +9,7 @@
 
 MESH = pl.DeviceIdType.MESH
 HALVES = 2
+PIECES = 4
 WIDTH = 512
 
 
@@ -38,6 +39,11 @@
     def lines(h):
         return pl.ds(h * piece, piece)
 
+    def bits(p):
+        return pl.ds(p * (rows // PIECES), rows // PIECES)
+
+    per_half = PIECES // HALVES
+
     def order(i):
         return i // 2 + (panels // 2) * lax.rem(i, 2)
 
@@ -52,43 +58,48 @@
     greet(ro=1 - core)
     pl.semaphore_wait(bar, 2 * n - 1)
 
-    def a0_copy(h, delta, direct):
+    def a0_copy(p, delta, direct):
         q = wrap(x + delta)
-        dst = a_all.at[2, lines(h), cols(q)] if direct else a_way.at[delta - 1, h]
-        return pltpu.make_async_remote_copy(
-            a_ref.at[lines(h), cols(q)], dst, a0_send.at[h, delta - 1], a0_recv.at[h, delta - 1],
+        dst = a_all.at[2, bits(p), cols(q)] if direct else a_way.at[delta - 1, p]
+        return pltpu.make_async_remote_copy(
+            a_ref.at[bits(p), cols(q)], dst, a0_send.at[p, delta - 1], a0_recv.at[p, delta - 1],
             device_id={"co": q}, device_id_type=MESH)
 
-    def a_local(h):
-        return pltpu.make_async_copy(a_ref.at[lines(h), cols(x)], a_all.at[2, lines(h), cols(x)], local_sem.at[h])
-
-    for h in range(HALVES):
+    def a_local():
+        return pltpu.make_async_copy(a_ref.at[:, cols(x)], a_all.at[2, :, cols(x)], local_sem.at[0])
+
+    def a0_start(p):
         @pl.when(diagonal)
         def _():
-            a_local(h).start()
             for delta in (1, 3, 2):
-                a0_copy(h, delta, True).start()
+                a0_copy(p, delta, True).start()
         @pl.when(jnp.logical_not(diagonal))
         def _():
             for delta in (1, 3, 2):
-                a0_copy(h, delta, False).start()
-
-    def a1_copy(h, off, src):
+                a0_copy(p, delta, False).start()
+
+    for p in range(PIECES):
+        a0_start(p)
+    @pl.when(diagonal)
+    def _():
+        a_local().start()
+
+    def a1_copy(p, off, src):
         slot = slot_of(off)
         return pltpu.make_async_remote_copy(
-            src, a_all.at[slot, lines(h), cols(x)], a1_send.at[h, off - 1], a1_recv.at[slot, h],
+            src, a_all.at[slot, bits(p), cols(x)], a1_send.at[p, off - 1], a1_recv.at[slot, p],
             device_id={"ri": wrap(y - off + n)}, device_id_type=MESH)
 
-    def a1_start(h, off):
+    def a1_start(p, off):
         delta = wrap(x - y + off + n)
         @pl.when(delta == 0)
         def _():
-            a1_copy(h, off, a_ref.at[lines(h), cols(x)]).start()
+            a1_copy(p, off, a_ref.at[bits(p), cols(x)]).start()
         for e in range(1, n):
             @pl.when(delta == e)
             def _():
-                a0_copy(h, e, False).wait_recv()
-                a1_copy(h, off, a_way.at[e - 1, h]).start()
+                a0_copy(p, e, False).wait_recv()
+                a1_copy(p, off, a_way.at[e - 1, p]).start()
 
     def b_copy(p):
         return pltpu.make_async_remote_copy(
@@ -117,20 +128,25 @@
             view, view, a2_send.at[slot, h, kind], a2_recv.at[slot, h, kind],
             device_id={"co": wrap(x + (1, n - 1, 1, n - 1, 2)[kind])}, device_id_type=MESH)
 
+    def passed_on(slot, h):
+        return slot == 3 or (slot < 2 and h == 0)
+
     def a2_start(slot, h):
-        if slot == 2:
+        for p in range(h * per_half, (h + 1) * per_half):
+            if slot == 2:
+                for e in range(1, n):
+                    @pl.when(wrap(x - y + n) == e)
+                    def _():
+                        a0_copy(p, e, False).wait_recv()
+            else:
+                a1_copy(p, (2 * slot + 1 if slot < 2 else 2), a_way.at[0, p]).wait_recv()
+        if slot == 2 and h == 0:
             @pl.when(diagonal)
             def _():
-                a_local(h).wait()
-            for e in range(1, n):
-                @pl.when(wrap(x - y + n) == e)
-                def _():
-                    a0_copy(h, e, False).wait_recv()
-        else:
-            a1_copy(h, (2 * slot + 1 if slot < 2 else 2), a_way.at[0, h]).wait_recv()
+                a_local().wait()
         a2_copy(slot, h, 0).start()
         a2_copy(slot, h, 1).start()
-        if slot != 3:
+        if not passed_on(slot, h):
             a2_copy(slot, h, 4).start()
 
     def relay(slot, h):
@@ -138,19 +154,20 @@
             a2_copy(slot, h, kind).wait_recv()
             a2_copy(slot, h, kind + 2).start()
 
-    for off in (2, 1, 3):
-        a1_start(0, off)
-    a2_start(3, 0)
-    for off in (2, 1, 3):
-        a1_start(1, off)
+    for h in range(HALVES):
+        for p in range(h * per_half, (h + 1) * per_half):
+            for off in (2, 1, 3):
+                a1_start(p, off)
+        if h == 0:
+            a2_start(3, 0)
     relay(3, 0)
     a2_start(3, 1)
 
     hooks = {
-        (0, 1): [lambda: relay(3, 1)],
-        (0, 2): [lambda: a2_start(0, 0), lambda: a2_start(1, 0)],
-        (0, 4): [lambda: a2_start(0, 1), lambda: a2_start(1, 1)],
-        (1, 1): [lambda: a2_start(2, 0), lambda: a2_start(2, 1)],
+        (0, 3): [lambda: relay(3, 1), lambda: a2_start(0, 0), lambda: a2_start(1, 0)],
+        (1, 3): [lambda: relay(0, 0)],
+        (1, 6): [lambda: relay(1, 0)],
+        (1, 7): [lambda: a2_start(0, 1), lambda: a2_start(1, 1), lambda: a2_start(2, 0), lambda: a2_start(2, 1)],
     }
 
     b_copy(0).wait_recv()
@@ -177,7 +194,7 @@
     for u, (kind, h) in enumerate(units):
         waits = {"far": [(3, h)], "near": [(0, h), (1, h)], "own": [(2, g) for g in range(HALVES)]}[kind]
         for slot, g in waits:
-            for k in (2, 3) if slot == 3 else (0, 1, 4):
+            for k in (2, 3) if passed_on(slot, g) else (0, 1, 4):
                 a2_copy(slot, g, k).wait_recv()
 
         def step(i, _, u=u, kind=kind, h=h):
@@ -249,12 +266,13 @@
 
     lax.fori_loop(0, panels, finish, 0)
 
+    for p in range(PIECES):
+        for delta in range(1, n):
+            a0_copy(p, delta, False).wait_send()
+            a1_copy(p, delta, a_way.at[0, p]).wait_send()
     for h in range(HALVES):
-        for delta in range(1, n):
-            a0_copy(h, delta, False).wait_send()
-            a1_copy(h, delta, a_way.at[0, h]).wait_send()
         for slot in range(n):
-            for kind in (0, 1, 2, 3) if slot == 3 else (0, 1, 4):
+            for kind in (0, 1, 2, 3) if passed_on(slot, h) else (0, 1, 4):
                 a2_copy(slot, h, kind).wait_send()
 
     def drain(p, _):
@@ -300,8 +318,8 @@
                 pltpu.VMEM((2, HALVES, panels, piece, WIDTH), f32),
                 pltpu.VMEM((rows, width), f32),
                 pltpu.VMEM((rows, width), bf16),
-                pltpu.VMEM((n - 1, HALVES, piece, depth // n), bf16),
-                dma((HALVES, n - 1)), dma((HALVES, n - 1)), dma((HALVES, n - 1)), dma((n, HALVES)), dma((n, HALVES, 5)), dma((n, HALVES, 5)), dma((HALVES,)),
+                pltpu.VMEM((n - 1, PIECES, rows // PIECES, depth // n), bf16),
+                dma((PIECES, n - 1)), dma((PIECES, n - 1)), dma((PIECES, n - 1)), dma((n, PIECES)), dma((n, HALVES, 5)), dma((n, HALVES, 5)), dma((1,)),
                 dma((panels,)), dma((panels,)), dma((2, 2)),
                 dma((HALVES, panels)), dma((HALVES, panels)), dma((2, HALVES, panels)), dma((2, HALVES, panels)),
                 dma((panels,)),

time: 208 us -> 204 us (0.981)
  Pallas kernels: 202 us -> 199 us
    pallas_call x1, Pallas kernels: 202 us -> 199 us  [block(): pl.pallas_call(functools.partial(kernel, n), out_shape=(jax.ShapeDtypeStr...]
where the time goes in v3:
time: 204 us; the launch traced here: 203 us
  Pallas kernels  199 us (98%)
  local copies, waits for them, and re-layouts  3.13 us (2%)
    pallas_call x1, Pallas kernels, block(): pl.pallas_call(functools.partial(kernel, n), out_shape=(jax.ShapeDtypeStr...  199 us

profile of v3, /device:TPU:97, one launch (start us, length us, event | category | flops | bytes accessed | tf_op | source)
XLA Modules:
  0.0 202.6 jit_solution(7684828463079747251)
XLA Ops:
  0.0 199.5 %shard_map.28 = (bf16[256,4096]{1,0:T(8,128)(2,1)}, bf16[3072,4096]{1,0:T(8,128)(2,1)}) custom-call(bf16[256,6144]{1,0:T(8,128)(2,1)} %a_ref.1, bf16[3072,4096]{1,0:T(8,128)(2,1)} %b_ref.1), custom_call_target="tpu_custom_call" | custom-call | tf_op jit(solution)/shard_map/pallas_call | solution.py:307
  199.5 3.1 %copy.4 = bf16[256,4096]{1,0:T(8,128)(2,1)} copy(bf16[256,4096]{1,0:T(8,128)(2,1)} %get-tuple-element.6) | data formatting | bytes 4194304
